TPU v7x, 32 devices: a whole 2x2x4 slice. The times are simulated.
32 devices in a mesh: groups: 2 (over x), chol: 16 (over z, y, core).
Axes of the slice: x: 2, y: 2, z: 4, core: 2. Of those that a mesh axis runs over, the one named last changes fastest.
Arguments:
- green_rows: bfloat16 [128, 65536], P('groups', 'chol'), parts along dimension 0, may hold values from -6 to 6
- factors: bfloat16 [5120, 65536], P(None, 'chol'), may hold values from -0.03125 to 0.03125
- noise_draws: float32 [128, 5120], P('groups', 'chol'), parts along dimension 0, may hold values from -6 to 6
Outputs:
- potential: float32 [128, 65536], P('groups', 'chol'), parts along dimension 0
- log_weight: float32 [128], P(('groups', 'chol')), parts along dimension 0
There are 2 independent parts, one for each index of `groups`. A program takes and returns all parts, laid end to end along the dimension named above; an argument that names none is the same for every part. Nothing has to cross between parts.
All inputs are finite; a program needn't handle non-finite values.
Results may differ from a plain program's by a relative error of at most 0.0029.
Values may be sent and summed in bfloat16 or wider, within the bound.
A program may use at most 128 MiB of HBM per device.

v0:
```python
import math

import jax
import jax.numpy as jnp
from jax import lax
from jax.sharding import PartitionSpec as P


def forward(rows_in, factors):
    return lax.dot_general(
        rows_in, factors, (((1,), (1,)), ((), ())), preferred_element_type=jnp.float32
    )


def weights_of(fields, capped, total_vectors):
    return jnp.sum(fields * capped - 0.5 * capped * capped, axis=1) / math.sqrt(total_vectors)


def per_device(green_rows, factors, noise_draws):
    total_vectors = factors.shape[0]
    partial_value = forward(green_rows, factors)
    forces = lax.psum_scatter(partial_value, "chol", scatter_dimension=1, tiled=True)
    capped = jnp.tanh(forces)
    fields = noise_draws - capped
    log_weight = lax.psum_scatter(
        weights_of(fields, capped, total_vectors), "chol", scatter_dimension=0, tiled=True
    )
    field_low = fields.astype(jnp.bfloat16)
    potential = jnp.dot(
        lax.all_gather(field_low, "chol", axis=1, tiled=True),
        factors,
        preferred_element_type=jnp.float32,
    )
    return (potential, log_weight)


def solution(mesh):
    return jax.shard_map(
        per_device,
        mesh=mesh,
        in_specs=(P("groups", "chol"), P(None, "chol"), P("groups", "chol")),
        out_specs=(P("groups", "chol"), P(("groups", "chol"))),
        check_vma=False,
    )
```

profile of v0, /device:TPU:1, one launch (start us, length us, event | category | flops | bytes accessed | tf_op | source)
XLA Modules:
  0.0 171.4 jit_solution(7765970410692516359)
XLA Ops:
  7.2 0.0 copy-start
  7.2 0.0 copy-start.2
  7.2 0.0 copy-start.1
  7.2 0.0 reduce-scatter.4.cloned.1.call-start
  7.2 1.0 copy-done
  8.2 18.5 %convolution_bitcast_fusion = f32[5120,64]{1,0:T(8,128)} fusion(bf16[64,4096]{1,0:T(8,128)(2,1)S(1)} %copy-done, bf16[5120,4096]{1,0:T(8,128)(2,1)} %param.4), kind=kOutput, calls=%fused_computation | convolution fusion | flops 2684354560 | bytes 43778048
  26.7 0.0 reduce-scatter.4.cloned.1.call-update
  26.7 0.0 copy-done.2
  26.7 0.6 dynamic-slice
  28.0 63.3 %reduce-scatter.4.cloned.1.call-done = f32[320,64]{1,0:T(8,128)} async-done(((f32[5120,64]{1,0:T(8,128)}), f32[320,64]{1,0:T(8,128)}) %reduce-scatter.4.cloned.1.call-update) | async-done | bytes 81936
  91.3 1.0 copy.8
  92.3 0.0 copy-done.1
  92.3 0.1 fusion.1
  92.5 23.7 %all-gather = bf16[16,320,64]{1,2,0:T(8,128)(2,1)S(1)} all-gather(bf16[1,320,64]{1,2,0:T(8,128)(2,1)S(1)} %get-tuple-element.3), channel_id=1, replica_groups=mesh['groups'=2,'chol'=16] {'chol'}, dimensions={0}, use_global_device_ids=true | all-gather | bytes 696320 | tf_op jit(solution)/shard_map/all_gather | solution.py:30
  116.2 0.5 copy.6
  116.7 0.6 reshape.5
  117.3 17.7 %fusion.3 = f32[64,4096]{1,0:T(8,128)} fusion(bf16[5120,64]{0,1:T(8,128)(2,1)S(1)} %reshape.5, bf16[5120,4096]{1,0:T(8,128)(2,1)} %param.4), kind=kOutput, calls=%fused_computation.7 | convolution fusion | flops 2684354560 | bytes 43646976 | tf_op jit(solution)/shard_map/dot_general | solution.py:29
  135.0 29.0 %all-reduce = f32[64]{0:T(128)S(1)} all-reduce(f32[64]{0:T(128)S(1)} %broadcast_multiply_fusion), channel_id=3, replica_groups=mesh['groups'=2,'chol'=16] {'chol'}, use_global_device_ids=true, to_apply=%region_2.0.clone | all-reduce | flops 64 | bytes 512
  164.0 0.6 dynamic-slice.1
  (1 shorter events, 0.0 us)
Async XLA Ops:
  7.2 1.0 copy-start
  7.2 19.5 %copy-start.2 = (u32[32]{0:T(128)S(1)}, u32[32]{0:T(128)}, u32[]{:S(2)}) copy-start(u32[32]{0:T(128)} %constant.9) | copy-start | bytes 388
  7.2 85.1 %copy-start.1 = (f32[64,320]{1,0:T(8,128)S(1)}, f32[64,320]{1,0:T(8,128)}, u32[]{:S(2)}) copy-start(f32[64,320]{1,0:T(8,128)} %param.5) | copy-start | bytes 245764
  7.2 84.1 %reduce-scatter.4.cloned.1.call-start = ((), (), s32[]{:S(2)}) async-start(), calls=%async_computation.1 | async-start | bytes 2785280
Sparse Core Ops, SparseCore 0:
  26.8 64.4 reduce-scatter.3
where the time goes:
time: 173 us; the launch traced here: 171 us
  waiting for transfers between devices  63.4 us (37%)
  blocking collectives  52.7 us (30%)
  matrix products  36.1 us (21%)
  between operations  14.7 us (8%)
  local copies, waits for them, and re-layouts  4.26 us (2%)
    unnamed x2, waiting for transfers between devices  63.4 us
    unnamed x1, blocking collectives  29 us
    all_gather x1, blocking collectives, per_device(): lax.all_gather(field_low, 'chol', axis=1, tiled=True)  23.7 us
    unnamed x1, matrix products  18.5 us
    dot_general x1, matrix products, per_device(): jnp.dot(lax.all_gather(field_low, 'chol', axis=1, tiled=True), factors, p...  17.7 us
    unnamed x10, local copies, waits for them, and re-layouts  3.8 us
  transfers between devices with their start and end apart: 1, of which 1 were waited for; matrix products, arithmetic and copies ran while one was open for 0% of the time, Pallas kernels for 0%

commit v1 on v0

v1 whole, which is shorter than its diff:
```python
import functools
import math

import jax
import jax.numpy as jnp
from jax import lax
from jax.experimental import pallas as pl
from jax.experimental.pallas import tpu as pltpu
from jax.sharding import PartitionSpec as P

MESH = pl.DeviceIdType.MESH
STAGES = 4


def flip(a, b, bits):
    total = 0
    for bit in range(bits):
        x = lax.rem(lax.div(a, 2**bit), 2)
        y = lax.rem(lax.div(b, 2**bit), 2) if not isinstance(b, int) else (b >> bit) & 1
        total = total + (x + y - 2 * x * y) * 2**bit
    return total


def kernel(n, pack, green, factors, noise, pot, logw, fac, own, d2d_out, d2d_in, rs_in, ag, nz,
           lhs, lw, lws, fac_sem, ds, dr, rs, rr, gs, gr, fs, fr, ls, lr, ps, pr):
    chips = n // 2
    bits = chips.bit_length() - 1
    total = factors.shape[0]
    nv = total // n
    half = nv // pack
    walkers = green.shape[0]
    me = lax.axis_index("chol")
    chip, core = lax.div(me, 2), lax.rem(me, 2)
    other = 1 - core
    partner = chip * 2 + other

    def peer(k):
        return flip(chip, k, bits) * 2 + core

    def load(i):
        k = chips - 1 - i
        rows = pl.ds(pl.multiple_of(flip(chip, k, bits) * (2 * nv), 2 * nv), 2 * nv)
        return pltpu.make_async_copy(factors.at[rows, :], fac.at[rows, :], fac_sem.at[k])

    def start_load(i, c):
        load(i).start()
        return c

    lax.fori_loop(0, chips, start_load, 0)

    barrier = pltpu.get_barrier_semaphore()
    pl.semaphore_signal(barrier, inc=1, device_id={"chol": partner}, device_id_type=MESH)

    def greet(k, c):
        pl.semaphore_signal(barrier, inc=1, device_id={"chol": peer(k)}, device_id_type=MESH)
        return c

    lax.fori_loop(1, chips, greet, 0)
    turned = noise[...].T
    nz[...] = jnp.concatenate([turned[j * half:(j + 1) * half] for j in range(pack)], axis=1)
    pl.semaphore_wait(barrier, chips)

    def remote(src, dst, s, r, to):
        return pltpu.make_async_remote_copy(
            src_ref=src, dst_ref=dst, send_sem=s, recv_sem=r,
            device_id={"chol": to}, device_id_type=MESH)

    def d2d(k):
        return remote(d2d_out.at[k], d2d_in.at[k], ds.at[k], dr.at[k], partner)

    def scatter(k):
        return remote(own.at[k], rs_in.at[k], rs.at[k], rr.at[k], peer(k))

    def partial(k, which):
        base = (flip(chip, k, bits) * 2 + which) * nv
        parts = []
        for j in range(pack):
            rows = pl.ds(pl.multiple_of(base + j * half, 16), half)
            parts.append(lax.dot_general(fac[rows, :], green[...], (((1,), (1,)), ((), ())),
                                         preferred_element_type=jnp.float32))
        return jnp.concatenate(parts, axis=1) if pack > 1 else parts[0]

    def finish(k):
        d2d(k).wait_recv()
        own[k] = own[k] + d2d_in[k]

    def step(i, c):
        k = chips - 1 - i
        load(i).wait()
        d2d_out[k] = partial(k, other)
        d2d(k).start()

        @pl.when(i > 0)
        def _():
            finish(k + 1)
            scatter(k + 1).start()

        own[k] = partial(k, core)
        return c

    lax.fori_loop(0, chips, step, 0)
    finish(0)

    def gather_sum(k, acc):
        scatter(k).wait_recv()
        return acc + rs_in[k]

    forces = lax.fori_loop(1, chips, gather_sum, own[0])
    capped = jnp.tanh(forces)
    fields = nz[...] - capped

    def spread(k):
        mine = ag.at[0, core]
        return remote(mine, ag.at[k, core], gs.at[k], gr.at[k], peer(k))

    def forward(k):
        return remote(ag.at[k, core], ag.at[k, core], fs.at[k], fr.at[k], partner)

    def forward_in(k):
        return remote(ag.at[k, other], ag.at[k, other], fs.at[k], fr.at[k], partner)

    def tell(k):
        return remote(lw.at[0], lw.at[k], ls.at[k], lr.at[k], peer(k))

    pair_sum = remote(lws.at[0], lws.at[1], ps, pr, partner)

    ag[0, core] = fields.astype(jnp.bfloat16)
    forward(0).start()

    def start_spread(k, c):
        spread(k).start()
        return c

    lax.fori_loop(1, chips, start_spread, 0)
    row = jnp.sum(fields * capped - 0.5 * capped * capped, axis=0, keepdims=True)
    lw[0] = jnp.broadcast_to(row, lw.shape[1:])

    def start_tell(k, c):
        tell(k).start()
        return c

    lax.fori_loop(1, chips, start_tell, 0)

    per_stage = chips // STAGES
    deep = total // STAGES
    own_stage = lax.div(chip, per_stage)
    cols = pot.shape[1]
    width = min(512, cols // 2)
    halves = cols // 2 // width

    def pull(s):
        def one(k, c):
            spread(k).wait_recv()
            forward(k).start()
            return c
        lax.fori_loop(max(1, s * per_stage), (s + 1) * per_stage, one, 0)

    def settle(s):
        def one(k, c):
            forward_in(k).wait_recv()
            return c
        lax.fori_loop(s * per_stage, (s + 1) * per_stage, one, 0)

    pull(0)
    settle(0)
    for s in range(STAGES):
        plane = flip(own_stage, s, 2)
        blocks = []
        for m in range(per_stage):
            k = flip(plane * per_stage + m, chip, bits)
            for c in range(2):
                block = ag[k, c]
                for j in range(pack):
                    blocks.append(block[:, j * walkers:(j + 1) * walkers])
        lhs[...] = jnp.concatenate(blocks, axis=0).T
        rows = pl.ds(pl.multiple_of(plane * deep, deep), deep)

        def column(t, c, s=s, rows=rows):
            at = pl.ds(pl.multiple_of(t * width, width), width)
            value = jnp.dot(lhs[...], fac[rows, at], preferred_element_type=jnp.float32)
            pot[:, at] = value if s == 0 else pot[:, at] + value
            return c

        lax.fori_loop(0, halves, column, 0)
        if s + 1 < STAGES:
            pull(s + 1)
        if s == STAGES - 2:
            def add(k, acc):
                tell(k).wait_recv()
                return acc + lw[k]
            lws[0] = lax.fori_loop(1, chips, add, lw[0])
            pair_sum.start()
        lax.fori_loop(halves, 2 * halves, column, 0)
        if s + 1 < STAGES:
            settle(s + 1)

    pair_sum.wait()
    packed = lws[0, 0:1, :] + lws[1, 0:1, :]
    row = packed[:, 0:walkers]
    for j in range(1, pack):
        row = row + packed[:, j * walkers:(j + 1) * walkers]
    per = walkers // n
    wide = jnp.broadcast_to(row, (per, walkers))
    here = lax.broadcasted_iota(jnp.int32, (per, walkers), 1) == (
        me * per + lax.broadcasted_iota(jnp.int32, (per, walkers), 0))
    logw[...] = jnp.sum(jnp.where(here, wide, 0.0), axis=1, keepdims=True) / math.sqrt(total)

    d2d(0).wait_send()
    forward(0).wait_send()

    def drain(k, c):
        d2d(k).wait_send()
        scatter(k).wait_send()
        spread(k).wait_send()
        forward(k).wait_send()
        tell(k).wait_send()
        return c

    lax.fori_loop(1, chips, drain, 0)


def solution(mesh):
    n = mesh.shape["chol"]

    def per_device(green, factors, noise):
        walkers, cols = green.shape
        total = factors.shape[0]
        chips = n // 2
        pack = max(1, 128 // walkers)
        half, lanes = total // n // pack, walkers * pack
        vmem = pl.BlockSpec(memory_space=pltpu.VMEM)
        dma = pltpu.SemaphoreType.DMA
        block = pltpu.VMEM((chips, half, lanes), jnp.float32)
        pot, logw = pl.pallas_call(
            functools.partial(kernel, n, pack),
            out_shape=(jax.ShapeDtypeStruct((walkers, cols), jnp.float32),
                       jax.ShapeDtypeStruct((walkers // n, 1), jnp.float32)),
            in_specs=[vmem, pl.BlockSpec(memory_space=pl.ANY), vmem],
            out_specs=(vmem, vmem),
            scratch_shapes=[
                pltpu.VMEM(factors.shape, jnp.bfloat16),
                block, block, block, block,
                pltpu.VMEM((chips, 2, half, lanes), jnp.bfloat16),
                pltpu.VMEM((half, lanes), jnp.float32),
                pltpu.VMEM((walkers, total // STAGES), jnp.bfloat16),
                pltpu.VMEM((chips, 8, lanes), jnp.float32),
                pltpu.VMEM((2, 8, lanes), jnp.float32),
            ] + [dma((chips,))] * 11 + [dma, dma],
            compiler_params=pltpu.CompilerParams(
                collective_id=0, has_side_effects=True, vmem_limit_bytes=67043328),
        )(green, factors, noise)
        return pot, logw.reshape(-1)

    return jax.shard_map(
        per_device,
        mesh=mesh,
        in_specs=(P("groups", "chol"), P(None, "chol"), P("groups", "chol")),
        out_specs=(P("groups", "chol"), P(("groups", "chol"))),
        check_vma=False,
    )
```

time: 173 us -> 49.5 us (0.29)
  waiting for transfers between devices: 63.4 us -> 0 us
  blocking collectives: 52.7 us -> 0 us
  Pallas kernels: 0 us -> 45.1 us
  matrix products: 36.1 us -> 0 us
  between operations: 14.7 us -> 0.64 us
  local copies, waits for them, and re-layouts: 4.26 us -> 2.27 us
    unnamed x2 -> x0, waiting for transfers between devices: 63.4 us -> none
    pallas_call x0 -> x1, Pallas kernels: none -> 45.1 us  [per_device(): pl.pallas_call(functools.partial(kernel, n, pack), out_shape=(jax.ShapeDt...]
    unnamed x1 -> x0, blocking collectives: 29 us -> none
    all_gather x1 -> x0, blocking collectives: 23.7 us -> none  [per_device(): lax.all_gather(field_low, 'chol', axis=1, tiled=True)]
    unnamed x1 -> x0, matrix products: 18.5 us -> none
    dot_general x1 -> x0, matrix products: 17.7 us -> none  [per_device(): jnp.dot(lax.all_gather(field_low, 'chol', axis=1, tiled=True), factors, p...]
    unnamed x10 -> x1, local copies, waits for them, and re-layouts: 3.8 us -> 2.27 us
  transfers between devices with their start and end apart: 1 -> 0, of which waited for: 1 -> 0; matrix products, arithmetic and copies ran while one was open for 0% -> 0% of each run, Pallas kernels for 0% -> 0%
where the time goes in v1:
time: 49.5 us; the launch traced here: 49.3 us
  Pallas kernels  45.1 us (91%)
  local copies, waits for them, and re-layouts  2.27 us (5%)
  other arithmetic  1.3 us (3%)
  between operations  0.64 us (1%)
    pallas_call x1, Pallas kernels, per_device(): pl.pallas_call(functools.partial(kernel, n, pack), out_shape=(jax.ShapeDt...  45.1 us
    unnamed x1, local copies, waits for them, and re-layouts  2.27 us
    pallas_call x1, other arithmetic, per_device(): pl.pallas_call(functools.partial(kernel, n, pack), out_shape=(jax.ShapeDt...  1.3 us

profile of v1, /device:TPU:1, one launch (start us, length us, event | category | flops | bytes accessed | tf_op | source)
XLA Modules:
  0.0 49.3 jit_solution(6570017924000528746)
XLA Ops:
  0.6 45.1 %shard_map.50 = (f32[64,4096]{1,0:T(8,128)}, f32[4,1]{1,0:T(4,128)}) custom-call(bf16[64,4096]{1,0:T(8,128)(2,1)} %green.1, bf16[5120,4096]{1,0:T(8,128)(2,1)} %factors.1, f32[64,320]{1,0:T(8,128)} %noise.1), custom_call_target="tpu_custom_call" | custom-call | tf_op jit(solution)/shard_map/pallas_call | solution.py:234
  45.8 1.3 %reduce = f32[4]{0:T(128)} reduce(f32[4,1]{1,0:T(4,128)} %get-tuple-element.5, f32[]{:T(128)} %constant), dimensions={1}, to_apply=%get-tuple-element.5.reduce_sub_computation | reduce | bytes 36 | tf_op jit(solution)/shard_map/pallas_call | solution.py:234
  47.1 2.3 %copy.6 = f32[64,4096]{1,0:T(8,128)} copy(f32[64,4096]{1,0:T(8,128)} %get-tuple-element.8) | data formatting | bytes 2097152

commit v2 on v1

--- a/solution.py
+++ b/solution.py
@@ -200,10 +200,13 @@
     for j in range(1, pack):
         row = row + packed[:, j * walkers:(j + 1) * walkers]
     per = walkers // n
-    wide = jnp.broadcast_to(row, (per, walkers))
-    here = lax.broadcasted_iota(jnp.int32, (per, walkers), 1) == (
-        me * per + lax.broadcasted_iota(jnp.int32, (per, walkers), 0))
-    logw[...] = jnp.sum(jnp.where(here, wide, 0.0), axis=1, keepdims=True) / math.sqrt(total)
+    lane = lax.broadcasted_iota(jnp.int32, (1, walkers), 1)
+    spot = lax.broadcasted_iota(jnp.int32, (1, per), 1)
+    mine = jnp.zeros((1, per), jnp.float32)
+    for j in range(per):
+        one = jnp.sum(jnp.where(lane == me * per + j, row, 0.0), axis=1, keepdims=True)
+        mine = jnp.where(spot == j, one, mine)
+    logw[...] = (mine / math.sqrt(total)).reshape(per)
 
     d2d(0).wait_send()
     forward(0).wait_send()
@@ -234,7 +237,7 @@
         pot, logw = pl.pallas_call(
             functools.partial(kernel, n, pack),
             out_shape=(jax.ShapeDtypeStruct((walkers, cols), jnp.float32),
-                       jax.ShapeDtypeStruct((walkers // n, 1), jnp.float32)),
+                       jax.ShapeDtypeStruct((walkers // n,), jnp.float32)),
             in_specs=[vmem, pl.BlockSpec(memory_space=pl.ANY), vmem],
             out_specs=(vmem, vmem),
             scratch_shapes=[
@@ -249,7 +252,7 @@
             compiler_params=pltpu.CompilerParams(
                 collective_id=0, has_side_effects=True, vmem_limit_bytes=67043328),
         )(green, factors, noise)
-        return pot, logw.reshape(-1)
+        return pot, logw
 
     return jax.shard_map(
         per_device,

time: 49.5 us -> 49.3 us (level)
  other arithmetic: 1.3 us -> 0 us
  local copies, waits for them, and re-layouts: 2.27 us -> 3.38 us
    pallas_call x1 -> x0, other arithmetic: 1.3 us -> none  [per_device(): pl.pallas_call(functools.partial(kernel, n, pack), out_shape=(jax.ShapeDt...]
    unnamed x1 -> x2, local copies, waits for them, and re-layouts: 2.27 us -> 3.38 us
where the time goes in v2:
time: 49.3 us; the launch traced here: 49.1 us
  Pallas kernels  45.1 us (91%)
  local copies, waits for them, and re-layouts  3.38 us (7%)
  between operations  0.64 us (1%)
    pallas_call x1, Pallas kernels, per_device(): pl.pallas_call(functools.partial(kernel, n, pack), out_shape=(jax.ShapeDt...  45.1 us
    unnamed x2, local copies, waits for them, and re-layouts  3.38 us

profile of v2, /device:TPU:1, one launch (start us, length us, event | category | flops | bytes accessed | tf_op | source)
XLA Modules:
  0.0 49.1 jit_solution(6838492071618620722)
XLA Ops:
  0.6 45.1 %shard_map.50 = (f32[64,4096]{1,0:T(8,128)}, f32[4]{0:T(128)}) custom-call(bf16[64,4096]{1,0:T(8,128)(2,1)} %green.1, bf16[5120,4096]{1,0:T(8,128)(2,1)} %factors.1, f32[64,320]{1,0:T(8,128)} %noise.1), custom_call_target="tpu_custom_call" | custom-call | tf_op jit(solution)/shard_map/pallas_call | solution.py:237
  45.8 2.3 %copy.7 = f32[64,4096]{1,0:T(8,128)} copy(f32[64,4096]{1,0:T(8,128)} %get-tuple-element.4) | data formatting | bytes 2097152
  48.0 1.1 %copy.8 = f32[4]{0:T(128)} copy(f32[4]{0:T(128)} %get-tuple-element.5) | data formatting | bytes 32
